TPU v7x, 32 devices: a whole 2x2x4 slice. The times are simulated.
32 devices in a mesh: sky: 8 (over z, y), band: 4 (over x, core).
Axes of the slice: x: 2, y: 2, z: 4, core: 2. Of those that a mesh axis runs over, the one named last changes fastest.
Arguments:
- magnitudes: float32 [4, 8, 16384], P('band', None, 'sky'), may hold values from -7 to 7
- weights: float32 [4, 8, 16384], P('band', None, 'sky'), may hold values from 0.25 to 4
- slots: int32 [4, 8, 16384], P('band', None, 'sky'), may hold values from 0 to 31, as said below
- block_fields: int32 [64, 32], P('sky'), may hold values from 0 to 4096, as said below
- owner: int32 [4096], replicated, may hold values from 0 to 7, as said below
- colors: int32 [4096], replicated, may hold values from 0 to 7
- color_terms: float32 [4, 4], replicated, may hold values from -0.25 to 0.25
Outputs:
- zero_points: float32 [4, 4096], P('band', 'sky')
- star_mags: float32 [4, 16384], P('band', 'sky')
- misfit: float32 [4, 4], P(None, 'band')
Inputs may be any that keep to these rules, and one draw needn't show every extreme that they name: `block_fields`: the live entries of each list come first, are distinct, and name fields owned by the block's own sky tile or by the tiles one index below or above it, cyclically over 8 tiles; the remaining entries equal 4096. A list holds 16 or more live entries, and every tile has a block with all 32 live. `owner`: each sky tile owns exactly 512 fields. `slots`: each observation names a live entry of its block's list.
All inputs are finite; a program needn't handle non-finite values.
Results may differ from a plain program's by a relative error of at most 0.00023.
Values sent between devices are 32-bit elements; how exact they have to be, the bound alone decides.
A program may use at most 64 MiB of HBM per device.

v0:
```python
import functools

import jax
import jax.numpy as jnp
from jax import lax
from jax.experimental import pallas as pl
from jax.experimental.pallas import tpu as pltpu
from jax.sharding import PartitionSpec as P

COLORS = 8
SWEEPS = 4
PRIOR_WEIGHT = 1.0
REACH = 2
HIGHEST = lax.Precision.HIGHEST
LANES = 128
EXTRA = 8
MESH = pl.DeviceIdType.MESH


def contract_lanes(left, right):
    dims = (((1,), (1,)), ((), ()))
    return lax.dot_general(left, right, dims, precision=HIGHEST, preferred_element_type=jnp.float32)


def mixing_of(terms_ref, bands):
    mixing = []
    for band in range(bands):
        total = terms_ref[band, 0]
        for other in range(1, bands):
            total = total + terms_ref[band, other]
        row = [terms_ref[band, other] for other in range(bands)]
        row[band] = (1.0 + row[band]) - total
        mixing.append(row)
    return mixing


def mixed(mixing, band, means):
    predicted = mixing[band][0] * means[0]
    for other in range(1, len(means)):
        predicted = predicted + mixing[band][other] * means[other]
    return predicted


def couple(bands, obs, list_len, rows, terms_ref, data_ref, places_ref, out_ref):
    blocks = data_ref.shape[3] // rows
    mixing = mixing_of(terms_ref, bands)
    row_band = lax.broadcasted_iota(jnp.int32, (LANES, LANES), 0) // list_len
    lane_band = lax.broadcasted_iota(jnp.int32, (LANES, LANES), 1) // list_len
    mix_grid = jnp.zeros((LANES, LANES), jnp.float32)
    for band in range(bands):
        for other in range(bands):
            here = (row_band == other) & (lane_band == band)
            mix_grid = jnp.where(here, mixing[band][other], mix_grid)
    full = []
    entry = lax.broadcasted_iota(jnp.int32, (list_len, rows), 0)
    for block in range(blocks):
        cols = pl.ds(block * rows, rows)
        one_hot, one_hot_mag, star_weight, means = [], [], [], []
        for band in range(bands):
            mags = data_ref[band, 0, :, cols]
            wts = data_ref[band, 1, :, cols]
            slots = places_ref[band, :, cols]
            scaled = wts * mags
            weight_sum = jnp.sum(wts, axis=0, keepdims=True)
            star_weight.append(weight_sum)
            means.append(jnp.sum(scaled, axis=0, keepdims=True) / weight_sum)
            hot = jnp.zeros((list_len, rows), jnp.float32)
            hot_mag = jnp.zeros((list_len, rows), jnp.float32)
            for k in range(obs):
                hit = slots[k : k + 1] == entry
                hot = hot + jnp.where(hit, wts[k : k + 1], 0.0)
                hot_mag = hot_mag + jnp.where(hit, scaled[k : k + 1], 0.0)
            one_hot.append(hot)
            one_hot_mag.append(hot_mag)
        rest = []
        shares = []
        for band in range(bands):
            rest.append(one_hot_mag[band] - one_hot[band] * mixed(mixing, band, means))
            shares.append(one_hot[band] / star_weight[band])
        hot_all = jnp.concatenate(one_hot, axis=0)
        share_all = jnp.concatenate(shares, axis=0)
        rest_all = jnp.concatenate(rest, axis=0)
        coupling = contract_lanes(share_all, hot_all) * mix_grid
        ones = jnp.ones((8, rows), jnp.float32)
        rest_row = contract_lanes(ones, rest_all)
        weight_row = contract_lanes(ones, hot_all)
        first = lax.broadcasted_iota(jnp.int32, (EXTRA, LANES), 0) == 0
        full.append(jnp.concatenate([coupling, jnp.where(first, rest_row, weight_row)], axis=0))
    split = bands // 2
    for part in range(split):
        pieces = []
        for half in range(2):
            band = half * split + part
            for block in range(blocks):
                pieces.append(full[block][:, band * list_len : (band + 1) * list_len])
        out_ref[part] = jnp.concatenate(pieces, axis=1)


def sweep_kernel(
    tiles, bands, obs, list_len, rows, row_count,
    window_ref, terms_ref, coupled_ref, pick_ref, color_ref,
    data_ref, data_places_ref, mags_ref, wts_ref, places_ref, chosen_ref,
    own_zp_ref, means_ref, sums_ref,
    kt, base, tot, rden, zp, move, lines, stage, sems,
):
    groups = row_count // 8
    pack = LANES // list_len
    split = bands // 2
    levels, places = pick_ref.shape[:2]
    depth = stage.shape[0]
    lane = lax.broadcasted_iota(jnp.int32, (8, LANES), 1)
    lane_wide = lax.broadcasted_iota(jnp.int32, (LANES + EXTRA, LANES), 1)

    def fetch(row, slot):
        return pltpu.make_async_copy(
            coupled_ref.at[pl.ds(row * (2 * split), 2 * split)], stage.at[slot], sems.at[slot]
        )

    for row in range(depth - 1):
        fetch(row, row).start()

    def unpack(row, carry):
        slot = lax.rem(row, depth)
        ahead = row + depth - 1

        @pl.when(ahead < row_count)
        def _():
            fetch(ahead, lax.rem(ahead, depth)).start()

        fetch(row, slot).wait()
        group = lax.div(row, 8)
        place = lax.rem(row, 8)
        for part in range(split):
            left = stage[slot, part]
            right = stage[slot, split + part]
            low = jnp.where(lane_wide < LANES // 2, left, pltpu.roll(right, LANES // 2, 1))
            high = jnp.where(lane_wide < LANES // 2, pltpu.roll(left, LANES // 2, 1), right)
            for band, value in ((part, low), (split + part, high)):
                start = (group * bands + band) * (LANES * 8) + place
                kt[pl.ds(start, LANES, stride=8), :] = value[0:LANES]
                base[band, pl.ds(row, 1), :] = value[LANES : LANES + 1]
                tot[band, pl.ds(row + 8, 1), :] = value[LANES + 1 : LANES + 2]
        return carry

    lax.fori_loop(0, row_count, unpack, 0)

    def rows_of(group):
        return pl.ds(pl.multiple_of(group * 8, 8), 8)

    def wrap():
        for band in range(bands):
            tot[band, 0:8, :] = tot[band, row_count : row_count + 8, :]
            tot[band, row_count + 8 : row_count + 16, :] = tot[band, 8:16, :]

    def gather(group, first, count, sums):
        for place in range(places):
            start = group * 8 + (8 + place - places // 2)
            near = [tot[band, pl.ds(start, 8), :] for band in range(bands)]
            for level in range(count):
                pick = pick_ref[first + level, place, rows_of(group), :]
                mask = pick < LANES
                lanes = pick & (LANES - 1)
                for band in range(bands):
                    index = 2 * band + level % 2
                    sums[index] = sums[index] + jnp.where(mask, take(near[band], lanes), 0.0)
        return sums

    def gathered(group):
        sums = []
        for band in range(bands):
            sums += [tot[band, pl.ds(pl.multiple_of(group * 8 + 8, 8), 8), :], jnp.zeros((8, LANES), jnp.float32)]
        sums = gather(group, 0, 2, sums)
        sums = lax.fori_loop(2, window_ref[0, 2], lambda level, sums: gather(group, level, 1, sums), sums)
        return [sums[2 * band] + sums[2 * band + 1] for band in range(bands)]

    def weigh(group, carry):
        for band, value in enumerate(gathered(group)):
            rden[band, rows_of(group), :] = 1.0 / (value + PRIOR_WEIGHT)
        return carry

    wrap()
    lax.fori_loop(0, groups, weigh, 0)
    zp[...] = jnp.zeros_like(zp)
    tot[:, 8 : row_count + 8, :] = base[...]
    wrap()

    def push(width, origin):
        def add(group, inner):
            here = [move[band, rows_of(group), :] for band in range(bands)]
            middle = pl.ds(pl.multiple_of(group * 8 + 8, 8), 8)
            sums = [tot[band, middle, :] for band in range(bands)]
            for entry in range(width):
                lanes = (lane & (LANES - list_len)) + (origin + entry)
                values = [take(here[band], lanes) for band in range(bands)]
                for band in range(bands):
                    for other in range(bands):
                        start = (group * bands + band) * (LANES * 8) + (other * list_len + origin + entry) * 8
                        rows = pl.ds(pl.multiple_of(start, 8), 8)
                        sums[band] = sums[band] + values[other] * kt[rows, :]
            for band in range(bands):
                tot[band, middle, :] = sums[band]
            return inner

        lax.fori_loop(0, groups, add, 0, unroll=2)

    halves = rows // LANES
    stars = mags_ref.shape[1]
    blocks = stars // rows
    tile_rows = blocks // pack
    mine = data_ref.shape[3] // rows
    my_tile, my_band = lax.axis_index("sky"), lax.axis_index("band")
    first = lax.rem(my_band * mine, pack)
    my_row = my_tile * tile_rows + lax.div(my_band * mine, pack)
    mixing = mixing_of(terms_ref, bands)
    lines[...] = jnp.zeros_like(lines)

    def spread(row, picks):
        return take(jnp.broadcast_to(row, (obs, LANES)), picks)

    def misfit_lines(sweep):
        partial = [jnp.zeros((obs, LANES), jnp.float32) for _ in range(bands)]
        for block in range(mine):
            for half in range(halves):
                cols = pl.ds(block * rows + half * LANES, LANES)
                left, means = [], []
                for band in range(bands):
                    wts = data_ref[band, 1, :, cols]
                    picks = data_places_ref[band, :, cols] + (first + block) * list_len
                    mags = data_ref[band, 0, :, cols] - spread(zp[band, pl.ds(my_row, 1), :], picks)
                    left.append(mags)
                    means.append(jnp.sum(wts * mags, axis=0, keepdims=True) / jnp.sum(wts, axis=0, keepdims=True))
                for band in range(bands):
                    wts = data_ref[band, 1, :, cols]
                    partial[band] = partial[band] + wts * (left[band] - mixed(mixing, band, means)) ** 2
        for band in range(bands):
            lines[pl.ds(sweep * bands + band, 1), :] = jnp.sum(partial[band], axis=0, keepdims=True)

    def step(number, carry):
        color_no = lax.rem(number, COLORS)

        def update(group, inner):
            rows = rows_of(group)
            now = color_ref[rows, :] == color_no
            for band, value in enumerate(gathered(group)):
                old = zp[band, rows, :]
                new = jnp.where(now, value * rden[band, rows, :], old)
                zp[band, rows, :] = new
                move[band, rows, :] = new - old
            return inner

        lax.fori_loop(0, groups, update, 0, unroll=2)

        @pl.when(color_no == COLORS - 1)
        def _():
            misfit_lines(lax.div(number, COLORS))

        low, high = window_ref[color_no, 0], window_ref[color_no, 1]
        widths = (list_len // 4, list_len * 3 // 8, list_len // 2)
        for index, width in enumerate(widths):
            fits = high - low <= width
            if index:
                fits = fits & (high - low > widths[index - 1])

            @pl.when(fits)
            def _(width=width):
                push(width, jnp.minimum(low, list_len - width))

        @pl.when(high - low > widths[-1])
        def _():
            lax.fori_loop(0, 2, lambda part, inner: (push(widths[-1], part * widths[-1]), inner)[1], 0)

        wrap()
        return carry

    lax.fori_loop(0, SWEEPS * COLORS, step, 0)
    sums_ref[...] = contract_lanes(jnp.ones((8, LANES), jnp.float32), lines[...])
    for block in range(blocks):
        row = zp[my_band, pl.ds(my_tile * tile_rows + block // pack, 1), :]
        for half in range(halves):
            cols = pl.ds(block * rows + half * LANES, LANES)
            wts = wts_ref[:, cols]
            picks = places_ref[:, cols] + block % pack * list_len
            left = wts * (mags_ref[:, cols] - spread(row, picks))
            means_ref[0:1, cols] = jnp.sum(left, axis=0, keepdims=True) / jnp.sum(wts, axis=0, keepdims=True)
    below = lax.broadcasted_iota(jnp.int32, (8, LANES), 0)
    close = jnp.zeros((8, LANES), jnp.float32)
    for offset in range(3):
        tile = lax.rem(my_tile + offset + tiles - 1, tiles)
        for row in range(tile_rows):
            value = zp[my_band, pl.ds(tile * tile_rows + row, 1), :]
            close = jnp.where(below == offset * tile_rows + row, jnp.broadcast_to(value, (8, LANES)), close)
    owned = own_zp_ref.shape[1]
    for row in range(chosen_ref.shape[0]):
        pick = chosen_ref[row]
        value = jnp.where(pick < LANES, take(close, pick & (LANES - 1)), 0.0)
        value = jnp.sum(value, axis=0, keepdims=True)
        width = min(LANES, owned - row * LANES)
        own_zp_ref[0:1, row * LANES : row * LANES + width] = value[:, 0:width]


def take(value, picks):
    return jnp.take_along_axis(value, picks, axis=1, mode="promise_in_bounds")


def sort_entries(list_len, fields, listed, color_ref):
    lane = lax.broadcasted_iota(jnp.int32, (8, LANES), 1)
    segment = lane & (LANES - list_len)
    live = listed < fields
    row_no, lane_no = listed // LANES, listed % LANES
    color = jnp.full((8, LANES), -1, jnp.int32)
    for row in range(color_ref.shape[0]):
        table = jnp.broadcast_to(color_ref[row : row + 1, :], (8, LANES))
        color = jnp.where(row_no == row, take(table, lane_no), color)
    color = jnp.where(live, color, -1)
    masks = jnp.concatenate([(color == c).astype(jnp.float32) for c in range(COLORS)], axis=0)
    source = lax.broadcasted_iota(jnp.int32, (LANES, LANES), 0)
    target = lax.broadcasted_iota(jnp.int32, (LANES, LANES), 1)
    same = (source // list_len) == (target // list_len)
    dims = (((1,), (0,)), ((), ()))
    before = (same & (source < target)).astype(jnp.float32)
    ranks = lax.dot_general(masks, before, dims, preferred_element_type=jnp.float32)
    counts = lax.dot_general(masks, same.astype(jnp.float32), dims, preferred_element_type=jnp.float32)
    rest = jnp.zeros((8, LANES), jnp.float32)
    room = [None] * COLORS
    for c in reversed(range(COLORS)):
        rest = rest + counts[c * 8 : c * 8 + 8]
        room[c] = list_len - rest
    end = jnp.zeros((8, LANES), jnp.float32)
    place = jnp.full((8, LANES), -1.0, jnp.float32)
    for c in range(COLORS):
        start = jnp.minimum(jnp.maximum(end, float(list_len * c // COLORS)), room[c])
        end = start + counts[c * 8 : c * 8 + 8]
        place = jnp.where(color == c, start + ranks[c * 8 : c * 8 + 8], place)
    place = place.astype(jnp.int32)
    sorted_fields = jnp.full((8, LANES), fields, jnp.int32)
    sorted_colors = jnp.full((8, LANES), -1, jnp.int32)
    for entry in range(list_len):
        picks = segment + entry
        hit = take(place, picks) == lane - segment
        sorted_fields = jnp.where(hit, take(listed, picks), sorted_fields)
        sorted_colors = jnp.where(hit, take(color, picks), sorted_colors)
    return place, sorted_fields, sorted_colors


def match(list_len, fields, lists_ref, rows_ref, pick_ref, color_ref):
    tiles, _, tile_rows, _ = lists_ref.shape
    pack = LANES // list_len
    levels, places, row_count, _ = pick_ref.shape
    lane = lax.broadcasted_iota(jnp.int32, (8, LANES), 1)
    for tile in range(tiles):
        start = tile * tile_rows
        rows_ref[8 + start : 8 + start + tile_rows, :] = lists_ref[tile, 0]
        color_ref[start : start + tile_rows, :] = lists_ref[tile, 1]
    rows_ref[0:8, :] = rows_ref[row_count : row_count + 8, :]
    rows_ref[row_count + 8 : row_count + 16, :] = rows_ref[8:16, :]

    def group_picks(group, carry):
        home = rows_ref[pl.ds(pl.multiple_of(group * 8 + 8, 8), 8), :]
        home = jnp.where(home < fields, home, -1)
        near = [rows_ref[pl.ds(group * 8 + 8 + place - places // 2, 8), :] for place in range(places)]
        found = [[] for _ in range(places)]
        for quarter in range(pack):
            picks = [jnp.full((8, LANES), LANES, jnp.int32) for _ in range(places)]
            for entry in range(list_len):
                source = quarter * list_len + entry
                for place in range(places):
                    other = jnp.broadcast_to(near[place][:, source : source + 1], (8, LANES))
                    picks[place] = jnp.where(other == home, source, picks[place])
            for place in range(places):
                found[place].append(picks[place])
        rows = pl.ds(pl.multiple_of(group * 8, 8), 8)
        for place in range(places):
            ranked = found[place]
            if place == places // 2:
                ranked = [jnp.where(pick == lane, LANES, pick) for pick in ranked]
            for turn in range(pack):
                for low in range(turn % 2, pack - 1, 2):
                    pair = ranked[low], ranked[low + 1]
                    ranked[low], ranked[low + 1] = jnp.minimum(*pair), jnp.maximum(*pair)
            for level in range(pack):
                pick_ref[level, place, rows, :] = ranked[level]
        return carry

    lax.fori_loop(0, row_count // 8, group_picks, 0)


def windows(list_len, pick_ref, color_ref, window_ref):
    levels, places, row_count, _ = pick_ref.shape
    lane = lax.broadcasted_iota(jnp.int32, (8, LANES), 1)
    position = (lane & (list_len - 1)).astype(jnp.float32)

    def rows_of(group):
        return pl.ds(pl.multiple_of(group * 8, 8), 8)

    def bounds(group, carry):
        lows, highs = carry
        color = color_ref[rows_of(group), :]
        new_lows, new_highs = [], []
        for c in range(COLORS):
            new_lows.append(jnp.minimum(lows[c], jnp.where(color == c, position, float(list_len))))
            new_highs.append(jnp.maximum(highs[c], jnp.where(color == c, position + 1.0, 0.0)))
        return new_lows, new_highs

    start = [jnp.full((8, LANES), float(list_len), jnp.float32)] * COLORS, [jnp.zeros((8, LANES), jnp.float32)] * COLORS
    lows, highs = lax.fori_loop(0, row_count // 8, bounds, start)
    lows = jnp.concatenate([jnp.min(value, axis=0, keepdims=True) for value in lows], axis=0)
    highs = jnp.concatenate([jnp.max(value, axis=0, keepdims=True) for value in highs], axis=0)
    lows = jnp.min(lows, axis=1, keepdims=True)
    highs = jnp.max(highs, axis=1, keepdims=True)
    deepest = jnp.full((8, LANES), 2.0, jnp.float32)
    for level in range(2, levels):
        def least(group, value, level=level):
            for place in range(places):
                value = jnp.minimum(value, pick_ref[level, place, rows_of(group), :])
            return value

        found = lax.fori_loop(0, row_count // 8, least, jnp.full((8, LANES), LANES, jnp.int32))
        deepest = jnp.where(found < LANES, level + 1.0, deepest)
    deepest = jnp.max(jnp.max(deepest, axis=0, keepdims=True), axis=1, keepdims=True)
    table = jnp.where(lane == 0, lows, jnp.where(lane == 1, highs, deepest))
    window_ref[...] = table.astype(jnp.int32)


def choose(tiles, fields, owner_ref, rows_ref, chosen_ref):
    field_rows = owner_ref.shape[0]
    tile_rows = (rows_ref.shape[0] - 16) // tiles
    my_tile = lax.axis_index("sky")
    lane = lax.broadcasted_iota(jnp.int32, (8, LANES), 1)
    below = lax.broadcasted_iota(jnp.int32, (8, LANES), 0)
    owned = owner_ref[...] == my_tile
    ones = owned.astype(jnp.float32)
    source = lax.broadcasted_iota(jnp.int32, (LANES, LANES), 0)
    target = lax.broadcasted_iota(jnp.int32, (LANES, LANES), 1)
    dims = (((1,), (0,)), ((), ()))
    inside = lax.dot_general(ones, (source < target).astype(jnp.float32), dims, preferred_element_type=jnp.float32)
    counts = lax.dot_general(ones, jnp.ones((LANES, LANES), jnp.float32), dims, preferred_element_type=jnp.float32)
    upper = lax.broadcasted_iota(jnp.int32, (field_rows, field_rows), 1)
    lower = lax.broadcasted_iota(jnp.int32, (field_rows, field_rows), 0)
    above = lax.dot_general((upper < lower).astype(jnp.float32), counts, dims, preferred_element_type=jnp.float32)
    rank = jnp.where(owned, (inside + above).astype(jnp.int32), -1)
    close = jnp.full((8, LANES), fields, jnp.int32)
    for offset in range(3):
        tile = lax.rem(my_tile + offset + tiles - 1, tiles)
        for row in range(tile_rows):
            value = rows_ref[pl.ds(8 + tile * tile_rows + row, 1), :]
            close = jnp.where(below == offset * tile_rows + row, jnp.broadcast_to(value, (8, LANES)), close)
    row_no, lane_no = close // LANES, close % LANES
    order = jnp.full((8, LANES), -1, jnp.int32)
    for row in range(field_rows):
        table = jnp.broadcast_to(rank[row : row + 1, :], (8, LANES))
        order = jnp.where(row_no == row, take(table, lane_no), order)
    own_rows = chosen_ref.shape[0]
    codes = [jnp.full((8, LANES), -1, jnp.int32) for _ in range(own_rows)]
    for entry in range(LANES):
        value = jnp.broadcast_to(order[:, entry : entry + 1], (8, LANES))
        for row in range(own_rows):
            codes[row] = jnp.where(value == row * LANES + lane, entry, codes[row])
    for row in range(own_rows):
        ranked = jnp.where(codes[row] >= 0, (below + 1).astype(jnp.float32), 0.0)
        last = jnp.max(ranked, axis=0, keepdims=True)
        keep = (ranked > 0.0) & (ranked == last)
        chosen_ref[row] = jnp.where(keep, codes[row], LANES)


def relabel(list_len, rows, block, offset, place_ref, slots_ref, out_ref):
    pack = LANES // list_len
    table = jnp.broadcast_to(place_ref[pl.ds(block // pack, 1), :], (slots_ref.shape[0], LANES))
    for half in range(rows // LANES):
        cols = pl.ds(offset + half * LANES, LANES)
        out_ref[:, cols] = take(table, slots_ref[:, cols] + block % pack * list_len)


def gather_kernel(
    tiles, bands, obs, list_len, rows, fields,
    terms_ref, tile_lists_ref, field_colors_ref, mags_ref, wts_ref, slots_ref, owner_ref,
    all_ref, pick_ref, color_ref, window_ref, chosen_ref, data_ref, data_places_ref, places_ref,
    rows_ref, own_ref, listed_ref, place_ref, sorted_ref, lists_ref, data_slots_ref,
    send_sems, recv_sems, early_send_sems, early_recv_sems,
):
    high_count = tiles // 2
    blocks = tile_lists_ref.shape[0]
    pack = LANES // list_len
    tile_rows = blocks // pack
    mine = blocks // bands
    width = mine * rows
    sky, band = lax.axis_index("sky"), lax.axis_index("band")
    high, low = sky // 2, sky % 2
    side, core = band // 2, band % 2
    to_low = {"sky": high * 2 + (1 - low)}
    to_side = {"band": (1 - side) * 2 + core}
    to_core = {"band": side * 2 + (1 - core)}
    barrier = pltpu.get_barrier_semaphore()
    tile_peers = [lax.rem(sky + step, tiles) for step in range(1, tiles)]
    band_peers = [lax.rem(band + step, bands) for step in range(1, bands)]
    for peer in tile_peers:
        pl.semaphore_signal(barrier, inc=1, device_id={"sky": peer}, device_id_type=MESH)
    for peer in band_peers:
        pl.semaphore_signal(barrier, inc=1, device_id={"band": peer}, device_id_type=MESH)

    listed_ref[...] = jnp.full((8, LANES), fields, jnp.int32)
    for row in range(tile_rows):
        pieces = [tile_lists_ref[row * pack + part : row * pack + part + 1, :] for part in range(pack)]
        listed_ref[row : row + 1, :] = jnp.concatenate(pieces, axis=1)
    place, sorted_fields, sorted_colors = sort_entries(list_len, fields, listed_ref[...], field_colors_ref)
    place_ref[...] = place
    sorted_ref[0] = sorted_fields[0:tile_rows]
    sorted_ref[1] = sorted_colors[0:tile_rows]
    lists_ref[sky] = sorted_ref[...]
    pl.semaphore_wait(barrier, tiles + bands - 2)

    def early(number, source, target, device):
        copy = pltpu.make_async_remote_copy(
            src_ref=source,
            dst_ref=target,
            send_sem=early_send_sems.at[number],
            recv_sem=early_recv_sems.at[number],
            device_id=device,
            device_id_type=MESH,
        )
        copy.start()
        return copy

    def columns(peer):
        return pl.ds(pl.multiple_of(peer * width, LANES), width)

    data_copies, list_copies = [], []
    for step, peer in enumerate(band_peers):
        cols = columns(peer)
        for kind, (source, target) in enumerate((
            (slots_ref, data_slots_ref.at[band]),
            (wts_ref, data_ref.at[band, 1]),
            (mags_ref, data_ref.at[band, 0]),
        )):
            data_copies.append(early(3 * step + kind, source.at[:, cols], target, {"band": peer}))
    for step, peer in enumerate(tile_peers):
        list_copies.append(early(3 * (bands - 1) + step, sorted_ref, lists_ref.at[sky], {"sky": peer}))
    data_ref[band, 0] = mags_ref[:, columns(band)]
    data_ref[band, 1] = wts_ref[:, columns(band)]
    data_slots_ref[band] = slots_ref[:, columns(band)]
    for block in range(blocks):
        relabel(list_len, rows, block, block * rows, place_ref, slots_ref, places_ref)
    for copy in data_copies:
        copy.wait_recv()
    for other in range(bands):
        for block in range(mine):
            source, target = data_slots_ref.at[other], data_places_ref.at[other]
            relabel(list_len, rows, band * mine + block, block * rows, place_ref, source, target)

    def tables():
        for copy in list_copies:
            copy.wait_recv()
        match(list_len, fields, lists_ref, rows_ref, pick_ref, color_ref)

    def more_tables():
        windows(list_len, pick_ref, color_ref, window_ref)
        choose(tiles, fields, owner_ref, rows_ref, chosen_ref)
        for copy in data_copies + list_copies:
            copy.wait_send()

    if high_count > 4:
        highs = [lax.rem(high + step, high_count) for step in range(1, high_count)]
        peers = [{"sky": peer * 2 + low} for peer in highs]
        couple(bands, obs, list_len, rows, terms_ref, data_ref, data_places_ref, own_ref)
        count = [0]

        def send(source, target, peer):
            copy = pltpu.make_async_remote_copy(
                src_ref=source,
                dst_ref=target,
                send_sem=send_sems.at[count[0]],
                recv_sem=recv_sems.at[count[0]],
                device_id=peer,
                device_id_type=MESH,
            )
            count[0] += 1
            copy.start()
            return copy

        def wait(copies):
            for copy in copies:
                copy.wait()

        mine = all_ref.at[high, low, side, core]
        copies = [send(own_ref, mine, peer) for peer in peers]
        all_ref[high, low, side, core] = own_ref[...]
        tables()
        more_tables()
        wait(copies)

        column = all_ref.at[:, low, side, core]
        first = all_ref.at[:, low, side, core, 0]
        second = all_ref.at[:, low, side, core, 1]
        copies = [send(first, first, to_low), send(second, second, to_side)]
        late = [send(column, column, to_core)]
        wait(copies)

        first = all_ref.at[:, :, side, core, 0]
        second = all_ref.at[:, low, :, core, 1]
        copies = [send(first, first, to_side), send(second, second, to_low)]
        for part in (all_ref.at[:, 1 - low, side, core, 0], all_ref.at[:, low, 1 - side, core, 1]):
            late.append(send(part, part, to_core))
        wait(copies)

        for part in (all_ref.at[:, :, 1 - side, core, 0], all_ref.at[:, 1 - low, :, core, 1]):
            late.append(send(part, part, to_core))
        wait(late)
        return

    chunks = high_count * 8
    lower, upper = high > 0, high < high_count - 1
    own_chunk = all_ref.at[high, low, side, core]
    couple(bands, obs, list_len, rows, terms_ref, data_ref, data_places_ref, own_chunk)
    def copy_of(kind, z, y, x, part, peer, landing):
        chunk = all_ref.at[z, y, x, core, part]
        number = ((z * 2 + y) * 2 + x) * 2 + part
        return pltpu.make_async_remote_copy(
            src_ref=chunk,
            dst_ref=chunk,
            send_sem=send_sems.at[kind * chunks + number],
            recv_sem=recv_sems.at[landing * chunks + number],
            device_id=peer,
            device_id_type=MESH,
        )

    def along(z, part, step):
        return copy_of((step + 1) // 2, z, low, side, part, {"sky": (high + step) * 2 + low}, 0)

    def across_x(z, y, part):
        return copy_of(2, z, y, side, part, to_side, 0)

    def across_y(z, x, part):
        return copy_of(3, z, low, x, part, to_low, 0)

    def over(z, y, x, part):
        return copy_of(4, z, y, x, part, to_core, 1)

    def arrived(z, y, x, part):
        copy_of(4, z, y, x, part, to_core, 0).wait_recv()

    ends = {-1: lower, 1: upper}

    def along_if(z, part, step):
        @pl.when(ends[step])
        def _():
            along(z, part, step).start()

    def first_hop(z, part):
        if part == 0:
            across_x(z, low, part).start()
        else:
            across_y(z, side, part).start()

    def second_hop(z, part):
        if part == 0:
            across_y(z, side, part).start()
        else:
            across_x(z, low, part).start()

    for part in range(2):
        along_if(high, part, 1)
        along_if(high, part, -1)
        first_hop(high, part)
    for part in range(2):
        second_hop(high, part)
        over(high, low, side, part).start()
    tables()

    def column_arrival(distance, part):
        for step in (-1, 1):
            z = high - step * distance
            here = z >= 0 if step == 1 else z < high_count

            @pl.when(here)
            def _(z=z, step=step):
                arrived(z, low, side, part)
                along_if(z, part, step)
                first_hop(z, part)
                second_hop(z, part)
                over(z, low, side, part).start()

    def at_distance(distance, action):
        if distance == 0:
            action(high)
            return
        for step in (-1, 1):
            z = high - step * distance

            @pl.when(z >= 0 if step == 1 else z < high_count)
            def _(z=z):
                action(z)

    def turn(z):
        arrived(z, low, 1 - side, 0)
        across_y(z, 1 - side, 0).start()
        over(z, low, 1 - side, 0).start()
        arrived(z, 1 - low, side, 1)
        across_x(z, 1 - low, 1).start()
        over(z, 1 - low, side, 1).start()

    def last(z):
        for y, x, part in ((1 - low, side, 0), (low, 1 - side, 1), (1 - low, 1 - side, 0), (1 - low, 1 - side, 1)):
            arrived(z, y, x, part)
            over(z, y, x, part).start()

    for distance in range(1, high_count):
        column_arrival(distance, 0)
        at_distance(distance - 1, turn)
        column_arrival(distance, 1)
        if distance > 1:
            at_distance(distance - 2, last)
        if distance == 1:
            more_tables()
    at_distance(high_count - 1, turn)
    for distance in range(max(high_count - 2, 0), high_count):
        at_distance(distance, last)

    for z in range(high_count):
        for y in range(2):
            for x in range(2):
                for part in range(2):
                    copy_of(4, z, y, x, part, to_core, 1).wait()
    for z in range(high_count):
        for part in range(2):
            for step in (-1, 1):
                passing = (z >= high) if step == -1 else (z <= high)

                @pl.when(ends[step] & passing)
                def _(z=z, part=part, step=step):
                    along(z, part, step).wait_send()

            for other in range(2):
                if part == 0:
                    across_y(z, other, part).wait_send()
                else:
                    across_x(z, other, part).wait_send()
            first = across_x(z, low, part) if part == 0 else across_y(z, side, part)
            first.wait_send()


def total_kernel(tiles, bands, scale, sums_ref, misfit_ref, all_sums, send_sems, recv_sems):
    my_tile, my_band = lax.axis_index("sky"), lax.axis_index("band")
    me = my_tile * bands + my_band
    peers = []
    for sky_step in range(tiles):
        for band_step in range(bands):
            if sky_step or band_step:
                peers.append({"sky": lax.rem(my_tile + sky_step, tiles), "band": lax.rem(my_band + band_step, bands)})
    barrier = pltpu.get_barrier_semaphore()
    for peer in peers:
        pl.semaphore_signal(barrier, inc=1, device_id=peer, device_id_type=MESH)
    all_sums[pl.ds(me, 1), :] = sums_ref[0:1, :]
    pl.semaphore_wait(barrier, len(peers))
    copies = []
    for number, peer in enumerate(peers):
        copy = pltpu.make_async_remote_copy(
            src_ref=sums_ref.at[0:1],
            dst_ref=all_sums.at[pl.ds(me, 1)],
            send_sem=send_sems.at[number],
            recv_sem=recv_sems.at[number],
            device_id=peer,
            device_id_type=MESH,
        )
        copy.start()
        copies.append(copy)
    for copy in copies:
        copy.wait()
    total = jnp.sum(all_sums[...], axis=0, keepdims=True) / scale
    lane = lax.broadcasted_iota(jnp.int32, (8, LANES), 1)
    picks = (lane * bands + my_band) & (LANES - 1)
    misfit_ref[...] = take(jnp.broadcast_to(total, (8, LANES)), picks)[0:1, 0:SWEEPS]


def body(magnitudes, weights, slots, block_fields, owner, colors, color_terms):
    bands = color_terms.shape[0]
    tiles = lax.axis_size("sky")
    _, obs, stars = magnitudes.shape
    blocks, list_len = block_fields.shape
    rows = stars // blocks
    fields = owner.shape[0]
    owned = fields // tiles
    mine = blocks // bands
    pack = LANES // list_len
    tile_rows = blocks // pack
    row_count = tiles * tile_rows
    vmem = pl.BlockSpec(memory_space=pltpu.VMEM)
    smem = pl.BlockSpec(memory_space=pltpu.SMEM)
    hbm = pl.BlockSpec(memory_space=pl.ANY)
    magnitudes, weights, slots = magnitudes[0], weights[0], slots[0]

    earlier = 3 * (bands - 1) + tiles - 1
    reach = 2 * (REACH * tile_rows + tile_rows - 1) + 1
    own_rows = -(-owned // LANES)
    part = (bands // 2, LANES + EXTRA, LANES)
    everyone = (tiles // 2, 2, bands // 2, 2) + part
    listed = (tiles, 2, tile_rows, LANES)
    if tiles > 8:
        sends = landings = tiles // 2 - 1 + 9
    else:
        sends, landings = 5 * tiles * 4, 2 * tiles * 4
    coupled, pick, entry_colors, window, chosen, data, data_places, places = pl.pallas_call(
        functools.partial(gather_kernel, tiles, bands, obs, list_len, rows, fields),
        out_shape=(
            jax.ShapeDtypeStruct(everyone, jnp.float32),
            jax.ShapeDtypeStruct((pack, reach, row_count, LANES), jnp.int32),
            jax.ShapeDtypeStruct((row_count, LANES), jnp.int32),
            jax.ShapeDtypeStruct((8, LANES), jnp.int32),
            jax.ShapeDtypeStruct((own_rows, 8, LANES), jnp.int32),
            jax.ShapeDtypeStruct((bands, 2, obs, mine * rows), jnp.float32),
            jax.ShapeDtypeStruct((bands, obs, mine * rows), jnp.int32),
            jax.ShapeDtypeStruct((obs, stars), jnp.int32),
        ),
        in_specs=[smem] + [vmem] * 6,
        out_specs=(vmem,) * 8,
        scratch_shapes=[
            pltpu.VMEM((row_count + 16, LANES), jnp.int32),
            pltpu.VMEM(part, jnp.float32),
            pltpu.VMEM((8, LANES), jnp.int32),
            pltpu.VMEM((8, LANES), jnp.int32),
            pltpu.VMEM(listed[1:], jnp.int32),
            pltpu.VMEM(listed, jnp.int32),
            pltpu.VMEM((bands, obs, mine * rows), jnp.int32),
            pltpu.SemaphoreType.DMA((sends,)),
            pltpu.SemaphoreType.DMA((landings,)),
            pltpu.SemaphoreType.DMA((earlier,)),
            pltpu.SemaphoreType.DMA((earlier,)),
        ],
        compiler_params=pltpu.CompilerParams(
            collective_id=0, has_side_effects=True, vmem_limit_bytes=60 * 1024 * 1024
        ),
        name="gather",
    )(color_terms, block_fields, colors.reshape(-1, LANES), magnitudes, weights, slots, owner.reshape(-1, LANES))
    coupled = coupled.reshape((-1,) + coupled.shape[-2:])

    big = (bands, row_count, LANES)
    depth = min(row_count, 16)
    own_zp, star_means, sums = pl.pallas_call(
        functools.partial(sweep_kernel, tiles, bands, obs, list_len, rows, row_count),
        out_shape=(
            jax.ShapeDtypeStruct((1, owned), jnp.float32),
            jax.ShapeDtypeStruct((1, stars), jnp.float32),
            jax.ShapeDtypeStruct((8, LANES), jnp.float32),
        ),
        in_specs=[smem, smem, hbm] + [vmem] * 8,
        out_specs=(vmem,) * 3,
        scratch_shapes=[
            pltpu.VMEM((row_count * bands * LANES, LANES), jnp.float32),
            pltpu.VMEM(big, jnp.float32),
            pltpu.VMEM((bands, row_count + 16, LANES), jnp.float32),
            pltpu.VMEM(big, jnp.float32),
            pltpu.VMEM(big, jnp.float32),
            pltpu.VMEM(big, jnp.float32),
            pltpu.VMEM((LANES, LANES), jnp.float32),
            pltpu.VMEM((depth, bands, LANES + EXTRA, LANES), jnp.float32),
            pltpu.SemaphoreType.DMA((depth,)),
        ],
        compiler_params=pltpu.CompilerParams(vmem_limit_bytes=60 * 1024 * 1024),
        name="sweeps",
    )(window, color_terms, coupled, pick, entry_colors, data, data_places, magnitudes, weights, places, chosen)

    devices = tiles * bands
    misfit = pl.pallas_call(
        functools.partial(total_kernel, tiles, bands, float(obs * stars * tiles)),
        out_shape=jax.ShapeDtypeStruct((1, SWEEPS), jnp.float32),
        in_specs=[vmem],
        out_specs=vmem,
        scratch_shapes=[
            pltpu.VMEM((devices, LANES), jnp.float32),
            pltpu.SemaphoreType.DMA((devices - 1,)),
            pltpu.SemaphoreType.DMA((devices - 1,)),
        ],
        compiler_params=pltpu.CompilerParams(collective_id=1, has_side_effects=True),
        name="total",
    )(sums)
    return own_zp, star_means, misfit.reshape(SWEEPS, 1)


def solution(mesh):
    in_specs = (
        P("band", None, "sky"),
        P("band", None, "sky"),
        P("band", None, "sky"),
        P("sky", None),
        P(),
        P(),
        P(),
    )
    out_specs = (P("band", "sky"), P("band", "sky"), P(None, "band"))
    return jax.shard_map(body, mesh=mesh, in_specs=in_specs, out_specs=out_specs, check_vma=False)
```

profile of v0, /device:TPU:0, one launch (start us, length us, event | category | flops | bytes accessed | tf_op | source)
XLA Modules:
  0.0 81.5 jit_solution(235597694126775593)
XLA Ops:
  0.6 40.0 %gather.1 = (f32[4,2,2,2,2,136,128]{6,5,4,3,2,1,0:T(8,128)}, s32[4,11,16,128]{3,2,1,0:T(8,128)}, s32[16,128]{1,0:T(8,128)}, s32[8,128]{1,0:T(8,128)}, s32[4,8,12...) custom-call(f32[4,4]{1,0:T(4,128)} %terms_ref.3, s32[8,32]{1,0:T(8,128)} %tile_lists_ref.1, ...), custom_call_target="tpu_custom_call" | custom-call | tf_op jit(solution)/shard_map/gather/pallas_call | solution.py:800
  40.6 30.5 %sweeps.1 = (f32[1,512]{1,0:T(1,128)}, f32[1,2048]{1,0:T(1,128)}, f32[8,128]{1,0:T(8,128)}) custom-call(s32[8,128]{1,0:T(8,128)} %get-tuple-element.14.window_ref, f32[4,4]{1,0:T(4,128)} %terms_ref.3, f32[64,136,128]{2,1,0:T(8,128)} %bitcast.7, s32[4,11,16,128]{3,2,1,0:T(8,128)} %get-tuple-element.16.pick_ref, s32[16,128]{1,0:T(8,128)} %get-tuple-element.17.color_ref, ...), custom_call_target="tpu_custom_call" | custom-call | tf_op jit(solution)/shard_map/sweeps/pallas_call | solution.py:836
  71.2 9.2 %total.1 = f32[1,4]{1,0:T(1,128)} custom-call(f32[8,128]{1,0:T(8,128)} %get-tuple-element.24.sums_ref), custom_call_target="tpu_custom_call" | custom-call | tf_op jit(solution)/shard_map/total/pallas_call | solution.py:861
  80.4 1.1 %copy.11 = f32[4,1]{0,1:T(1,128)} copy(f32[4,1]{0,1:T(1,128)} %bitcast.15) | data formatting | bytes 32
where the time goes:
time: 81.5 us
  Pallas kernels  79.7 us (98%)
  local copies, waits for them, and re-layouts  1.14 us (1%)
    pallas_call x1, Pallas kernels, body(): pl.pallas_call(functools.partial(gather_kernel, tiles, bands, obs, list_l...  40 us
    pallas_call x1, Pallas kernels, body(): pl.pallas_call(functools.partial(sweep_kernel, tiles, bands, obs, list_le...  30.5 us
    pallas_call x1, Pallas kernels, body(): pl.pallas_call(functools.partial(total_kernel, tiles, bands, float(obs *...  9.19 us

commit v1 on v0

--- a/solution.py
+++ b/solution.py
@@ -98,10 +98,10 @@
 
 def sweep_kernel(
     tiles, bands, obs, list_len, rows, row_count,
-    window_ref, terms_ref, coupled_ref, pick_ref, color_ref,
-    data_ref, data_places_ref, mags_ref, wts_ref, places_ref, chosen_ref,
+    window_ref, terms_ref, coupled_ref, pick_hbm_ref, color_ref,
+    data_ref, data_places_ref, mags_ref, wts_ref, places_ref, chosen_ref, homes_ref, ranked_ref,
     own_zp_ref, means_ref, sums_ref,
-    kt, base, tot, rden, zp, move, lines, stage, sems,
+    kt, base, tot, rden, zp, move, lines, pick_ref, pick_sem, wide, twice, ctot, crden, stage, sems,
 ):
     groups = row_count // 8
     pack = LANES // list_len
@@ -178,19 +178,15 @@
             rden[band, rows_of(group), :] = 1.0 / (value + PRIOR_WEIGHT)
         return carry
 
-    wrap()
-    lax.fori_loop(0, groups, weigh, 0)
     zp[...] = jnp.zeros_like(zp)
-    tot[:, 8 : row_count + 8, :] = base[...]
-    wrap()
-
-    def push(width, origin):
+
+    def push(width, origin, first_lane):
         def add(group, inner):
             here = [move[band, rows_of(group), :] for band in range(bands)]
             middle = pl.ds(pl.multiple_of(group * 8 + 8, 8), 8)
             sums = [tot[band, middle, :] for band in range(bands)]
             for entry in range(width):
-                lanes = (lane & (LANES - list_len)) + (origin + entry)
+                lanes = first_lane + entry
                 values = [take(here[band], lanes) for band in range(bands)]
                 for band in range(bands):
                     for other in range(bands):
@@ -202,6 +198,19 @@
             return inner
 
         lax.fori_loop(0, groups, add, 0, unroll=2)
+
+    def push_window(color_no, first_lane):
+        low, high = window_ref[color_no, 0], window_ref[color_no, 1]
+        widths = (list_len // 4, list_len * 3 // 8, list_len // 2)
+        for index, width in enumerate(widths):
+            fits = high - low <= width
+            if index:
+                fits = fits & (high - low > widths[index - 1])
+
+            @pl.when(fits)
+            def _(width=width):
+                origin = jnp.minimum(low, list_len - width)
+                push(width, origin, first_lane(origin))
 
     halves = rows // LANES
     stars = mags_ref.shape[1]
@@ -254,25 +263,110 @@
         def _():
             misfit_lines(lax.div(number, COLORS))
 
-        low, high = window_ref[color_no, 0], window_ref[color_no, 1]
-        widths = (list_len // 4, list_len * 3 // 8, list_len // 2)
-        for index, width in enumerate(widths):
-            fits = high - low <= width
-            if index:
-                fits = fits & (high - low > widths[index - 1])
-
-            @pl.when(fits)
-            def _(width=width):
-                push(width, jnp.minimum(low, list_len - width))
-
-        @pl.when(high - low > widths[-1])
+        segment = lane & (LANES - list_len)
+        push_window(color_no, lambda origin: segment + origin)
+
+        @pl.when(window_ref[color_no, 1] - window_ref[color_no, 0] > list_len // 2)
         def _():
-            lax.fori_loop(0, 2, lambda part, inner: (push(widths[-1], part * widths[-1]), inner)[1], 0)
+            def half(part, inner):
+                push(list_len // 2, part * (list_len // 2), segment + part * (list_len // 2))
+                return inner
+
+            lax.fori_loop(0, 2, half, 0)
 
         wrap()
         return carry
 
-    lax.fori_loop(0, SWEEPS * COLORS, step, 0)
+    def all_steps():
+        copy = pltpu.make_async_copy(pick_hbm_ref, pick_ref, pick_sem)
+        copy.start()
+        copy.wait()
+        wrap()
+        lax.fori_loop(0, groups, weigh, 0)
+        tot[:, 8 : row_count + 8, :] = base[...]
+        wrap()
+        lax.fori_loop(0, SWEEPS * COLORS, step, 0)
+
+    def compact(color_no):
+        picks = (lane // SLOTS) % pack * list_len + lane % SLOTS
+        picks = picks + jnp.minimum(window_ref[color_no, 0], list_len - SLOTS)
+        for group in range(2):
+            for band in range(bands):
+                wide[band, group * 8 : group * 8 + 8, :] = take(tot[band, group * 8 + 8 : group * 8 + 16, :], picks)
+        sums = []
+        for band in range(bands):
+            even = wide[band, pl.ds(0, 8, stride=2), :]
+            odd = wide[band, pl.ds(1, 8, stride=2), :]
+            value = jnp.where(lane < LANES // 2, even, odd)
+            twice[band, 0:8, :] = value
+            twice[band, 8:16, :] = value
+            sums += [value, jnp.zeros((8, LANES), jnp.float32)]
+
+        def add(first, count, sums):
+            for index in range(2 * AROUND + 1):
+                start = (index - AROUND) % 8
+                near = [twice[band, start : start + 8, :] for band in range(bands)]
+                for level in range(count):
+                    pick = ranked_ref[color_no, first + level, index]
+                    mask = pick < LANES
+                    lanes = pick & (LANES - 1)
+                    for band in range(bands):
+                        at = 2 * band + level % 2
+                        sums[at] = sums[at] + jnp.where(mask, take(near[band], lanes), 0.0)
+            return sums
+
+        sums = add(0, DEPTH - 1, sums)
+        sums = lax.fori_loop(DEPTH - 1, window_ref[0, 3], lambda level, sums: add(level, 1, sums), sums)
+        return [sums[2 * band] + sums[2 * band + 1] for band in range(bands)]
+
+    def compact_weigh(color_no, carry):
+        live = homes_ref[color_no] >= 0
+        for band, value in enumerate(compact(color_no)):
+            crden[color_no, band] = jnp.where(live, 1.0 / (value + PRIOR_WEIGHT), 0.0)
+        return carry
+
+    def compact_step(number, carry):
+        color_no = lax.rem(number, COLORS)
+        for band, value in enumerate(compact(color_no)):
+            new = value * crden[color_no, band]
+            change = new - ctot[color_no, band]
+            ctot[color_no, band] = new
+            wide[band, pl.ds(0, 8, stride=2), :] = change
+            wide[band, pl.ds(1, 8, stride=2), :] = change
+        below = lax.broadcasted_iota(jnp.int32, (8, LANES), 0)
+        origin = jnp.minimum(window_ref[color_no, 0], list_len - SLOTS)
+        first_lane = (below & 1) * (LANES // 2) + (lane // list_len) * SLOTS
+        own_lane = (first_lane + (lane & (list_len - 1)) - origin) & (LANES - 1)
+        for group in range(2):
+            now = color_ref[group * 8 : group * 8 + 8, :] == color_no
+            for band in range(bands):
+                change = wide[band, group * 8 : group * 8 + 8, :]
+                move[band, group * 8 : group * 8 + 8, :] = change
+                old = zp[band, group * 8 : group * 8 + 8, :]
+                zp[band, group * 8 : group * 8 + 8, :] = old + jnp.where(now, take(change, own_lane), 0.0)
+
+        @pl.when(color_no == COLORS - 1)
+        def _():
+            misfit_lines(lax.div(number, COLORS))
+
+        push_window(color_no, lambda start: first_lane + (start - origin))
+        return carry
+
+    if row_count == 16:
+        fast = window_ref[0, 3] <= DEPTH
+        for color_no in range(COLORS):
+            fast = fast & (window_ref[color_no, 1] - window_ref[color_no, 0] <= SLOTS)
+
+        @pl.when(fast)
+        def _():
+            lax.fori_loop(0, COLORS, compact_weigh, 0)
+            ctot[...] = jnp.zeros_like(ctot)
+            tot[:, 8 : row_count + 8, :] = base[...]
+            lax.fori_loop(0, SWEEPS * COLORS, compact_step, 0)
+
+        pl.when(jnp.logical_not(fast))(all_steps)
+    else:
+        all_steps()
     sums_ref[...] = contract_lanes(jnp.ones((8, LANES), jnp.float32), lines[...])
     for block in range(blocks):
         row = zp[my_band, pl.ds(my_tile * tile_rows + block // pack, 1), :]
@@ -419,6 +513,63 @@
     deepest = jnp.max(jnp.max(deepest, axis=0, keepdims=True), axis=1, keepdims=True)
     table = jnp.where(lane == 0, lows, jnp.where(lane == 1, highs, deepest))
     window_ref[...] = table.astype(jnp.int32)
+
+
+SLOTS = 16
+DEPTH = 3
+AROUND = 3
+
+
+def compact_tables(list_len, colors, rows_ref, color_ref, window_ref, homes_ref, ranked_ref, stage_ref, flags_ref):
+    lane = lax.broadcasted_iota(jnp.int32, (8, LANES), 1)
+    offsets = range(-AROUND, AROUND + 1)
+
+    def one_color(c, carry):
+        low = jnp.broadcast_to(window_ref[pl.ds(c, 1), :][:, 0:1], (8, LANES))
+        picks = (lane // SLOTS) % (LANES // list_len) * list_len + lane % SLOTS
+        picks = picks + jnp.minimum(low, list_len - SLOTS)
+        for group in range(2):
+            listed = rows_ref[8 + group * 8 : 16 + group * 8, :]
+            color = color_ref[group * 8 : group * 8 + 8, :]
+            stage_ref[group * 8 : group * 8 + 8, :] = take(jnp.where(color == c, listed, -1), picks)
+        even = stage_ref[pl.ds(0, 8, stride=2), :]
+        odd = stage_ref[pl.ds(1, 8, stride=2), :]
+        home = jnp.where(lane < LANES // 2, even, odd)
+        homes_ref[c] = home
+        stage_ref[0:8, :] = home
+        stage_ref[8:16, :] = home
+        near = [stage_ref[offset % 8 : offset % 8 + 8, :] for offset in offsets]
+        target = jnp.where(home >= 0, home, -2)
+        ranked = [[jnp.full((8, LANES), LANES, jnp.int32)] * (DEPTH + 1) for _ in offsets]
+        for block in range(LANES // SLOTS):
+            found = [jnp.full((8, LANES), LANES, jnp.int32) for _ in offsets]
+            for source in range(block * SLOTS, (block + 1) * SLOTS):
+                for index in range(len(offsets)):
+                    other = jnp.broadcast_to(near[index][:, source : source + 1], (8, LANES))
+                    found[index] = jnp.where(other == target, source, found[index])
+            found[AROUND] = jnp.where(found[AROUND] == lane, LANES, found[AROUND])
+            for index in range(len(offsets)):
+                rest = found[index]
+                for level in range(DEPTH + 1):
+                    kept = ranked[index][level]
+                    ranked[index][level] = jnp.minimum(kept, rest)
+                    rest = jnp.maximum(kept, rest)
+        flags = flags_ref[...]
+        for index in range(len(offsets)):
+            for level in range(DEPTH):
+                ranked_ref[c, level, index] = ranked[index][level]
+            flags = jnp.where(ranked[index][DEPTH - 1] < LANES, jnp.maximum(flags, float(DEPTH)), flags)
+            flags = jnp.where(ranked[index][DEPTH] < LANES, DEPTH + 1.0, flags)
+        flags_ref[...] = flags
+        return carry
+
+    lax.fori_loop(*colors, one_color, 0)
+
+
+def note_depth(window_ref, flags_ref):
+    lane = lax.broadcasted_iota(jnp.int32, (8, LANES), 1)
+    deepest = jnp.max(jnp.max(flags_ref[...], axis=0, keepdims=True), axis=1, keepdims=True)
+    window_ref[...] = jnp.where(lane == 3, deepest.astype(jnp.int32), window_ref[...])
 
 
 def choose(tiles, fields, owner_ref, rows_ref, chosen_ref):
@@ -474,7 +625,8 @@
     tiles, bands, obs, list_len, rows, fields,
     terms_ref, tile_lists_ref, field_colors_ref, mags_ref, wts_ref, slots_ref, owner_ref,
     all_ref, pick_ref, color_ref, window_ref, chosen_ref, data_ref, data_places_ref, places_ref,
-    rows_ref, own_ref, listed_ref, place_ref, sorted_ref, lists_ref, data_slots_ref,
+    homes_ref, ranked_ref,
+    pair_ref, flags_ref, rows_ref, own_ref, listed_ref, place_ref, sorted_ref, lists_ref, data_slots_ref,
     send_sems, recv_sems, early_send_sems, early_recv_sems,
 ):
     high_count = tiles // 2
@@ -553,9 +705,16 @@
 
     def more_tables():
         windows(list_len, pick_ref, color_ref, window_ref)
+        flags_ref[...] = jnp.full((8, LANES), DEPTH - 1.0, jnp.float32)
         choose(tiles, fields, owner_ref, rows_ref, chosen_ref)
         for copy in data_copies + list_copies:
             copy.wait_send()
+
+    def color_tables(start, stop):
+        args = rows_ref, color_ref, window_ref, homes_ref, ranked_ref, pair_ref, flags_ref
+        compact_tables(list_len, (start, stop), *args)
+        if stop == COLORS:
+            note_depth(window_ref, flags_ref)
 
     if high_count > 4:
         highs = [lax.rem(high + step, high_count) for step in range(1, high_count)]
@@ -585,6 +744,8 @@
         all_ref[high, low, side, core] = own_ref[...]
         tables()
         more_tables()
+        homes_ref[...] = jnp.zeros_like(homes_ref)
+        ranked_ref[...] = jnp.zeros_like(ranked_ref)
         wait(copies)
 
         column = all_ref.at[:, low, side, core]
@@ -710,7 +871,10 @@
             at_distance(distance - 2, last)
         if distance == 1:
             more_tables()
+        else:
+            color_tables(COLORS * (distance - 2) // (high_count - 1), COLORS * (distance - 1) // (high_count - 1))
     at_distance(high_count - 1, turn)
+    color_tables(COLORS * (high_count - 2) // (high_count - 1), COLORS)
     for distance in range(max(high_count - 2, 0), high_count):
         at_distance(distance, last)
 
@@ -797,7 +961,7 @@
         sends = landings = tiles // 2 - 1 + 9
     else:
         sends, landings = 5 * tiles * 4, 2 * tiles * 4
-    coupled, pick, entry_colors, window, chosen, data, data_places, places = pl.pallas_call(
+    coupled, pick, entry_colors, window, chosen, data, data_places, places, homes, ranked = pl.pallas_call(
         functools.partial(gather_kernel, tiles, bands, obs, list_len, rows, fields),
         out_shape=(
             jax.ShapeDtypeStruct(everyone, jnp.float32),
@@ -808,10 +972,14 @@
             jax.ShapeDtypeStruct((bands, 2, obs, mine * rows), jnp.float32),
             jax.ShapeDtypeStruct((bands, obs, mine * rows), jnp.int32),
             jax.ShapeDtypeStruct((obs, stars), jnp.int32),
+            jax.ShapeDtypeStruct((COLORS, 8, LANES), jnp.int32),
+            jax.ShapeDtypeStruct((COLORS, DEPTH, 2 * AROUND + 1, 8, LANES), jnp.int32),
         ),
         in_specs=[smem] + [vmem] * 6,
-        out_specs=(vmem,) * 8,
+        out_specs=(vmem,) * 10,
         scratch_shapes=[
+            pltpu.VMEM((16, LANES), jnp.int32),
+            pltpu.VMEM((8, LANES), jnp.float32),
             pltpu.VMEM((row_count + 16, LANES), jnp.int32),
             pltpu.VMEM(part, jnp.float32),
             pltpu.VMEM((8, LANES), jnp.int32),
@@ -840,7 +1008,7 @@
             jax.ShapeDtypeStruct((1, stars), jnp.float32),
             jax.ShapeDtypeStruct((8, LANES), jnp.float32),
         ),
-        in_specs=[smem, smem, hbm] + [vmem] * 8,
+        in_specs=[smem, smem, hbm, hbm] + [vmem] * 9,
         out_specs=(vmem,) * 3,
         scratch_shapes=[
             pltpu.VMEM((row_count * bands * LANES, LANES), jnp.float32),
@@ -850,12 +1018,18 @@
             pltpu.VMEM(big, jnp.float32),
             pltpu.VMEM(big, jnp.float32),
             pltpu.VMEM((LANES, LANES), jnp.float32),
+            pltpu.VMEM(pick.shape, jnp.int32),
+            pltpu.SemaphoreType.DMA,
+            pltpu.VMEM((bands, 16, LANES), jnp.float32),
+            pltpu.VMEM((bands, 16, LANES), jnp.float32),
+            pltpu.VMEM((COLORS, bands, 8, LANES), jnp.float32),
+            pltpu.VMEM((COLORS, bands, 8, LANES), jnp.float32),
             pltpu.VMEM((depth, bands, LANES + EXTRA, LANES), jnp.float32),
             pltpu.SemaphoreType.DMA((depth,)),
         ],
         compiler_params=pltpu.CompilerParams(vmem_limit_bytes=60 * 1024 * 1024),
         name="sweeps",
-    )(window, color_terms, coupled, pick, entry_colors, data, data_places, magnitudes, weights, places, chosen)
+    )(window, color_terms, coupled, pick, entry_colors, data, data_places, magnitudes, weights, places, chosen, homes, ranked)
 
     devices = tiles * bands
     misfit = pl.pallas_call(

time: 81.5 us -> 84 us (1.031)
  Pallas kernels: 79.7 us -> 81.6 us
    pallas_call x1, Pallas kernels: 40 us -> 42.6 us  [body(): pl.pallas_call(functools.partial(gather_kernel, tiles, bands, obs, list_l...]
    pallas_call x1, Pallas kernels: 30.5 us -> 28.1 us  [body(): pl.pallas_call(functools.partial(sweep_kernel, tiles, bands, obs, list_le...]
    pallas_call x1, Pallas kernels: 9.19 us -> 11 us  [body(): pl.pallas_call(functools.partial(total_kernel, tiles, bands, float(obs *...]
where the time goes in v1:
time: 84 us; the launch traced here: 83.4 us
  Pallas kernels  81.6 us (97%)
  local copies, waits for them, and re-layouts  1.14 us (1%)
    pallas_call x1, Pallas kernels, body(): pl.pallas_call(functools.partial(gather_kernel, tiles, bands, obs, list_l...  42.6 us
    pallas_call x1, Pallas kernels, body(): pl.pallas_call(functools.partial(sweep_kernel, tiles, bands, obs, list_le...  28.1 us
    pallas_call x1, Pallas kernels, body(): pl.pallas_call(functools.partial(total_kernel, tiles, bands, float(obs *...  11 us

profile of v1, /device:TPU:0, one launch (start us, length us, event | category | flops | bytes accessed | tf_op | source)
XLA Modules:
  0.0 83.4 jit_solution(13964249141447469335)
XLA Ops:
  0.6 42.6 %gather.1 = (f32[4,2,2,2,2,136,128]{6,5,4,3,2,1,0:T(8,128)}, s32[4,11,16,128]{3,2,1,0:T(8,128)}, s32[16,128]{1,0:T(8,128)}, s32[8,128]{1,0:T(8,128)}, s32[4,8,12...) custom-call(f32[4,4]{1,0:T(4,128)} %terms_ref.3, ...), custom_call_target="tpu_custom_call" | custom-call | tf_op jit(solution)/shard_map/gather/pallas_call | solution.py:964
  43.2 28.1 %sweeps.1 = (f32[1,512]{1,0:T(1,128)}, f32[1,2048]{1,0:T(1,128)}, f32[8,128]{1,0:T(8,128)}) custom-call(s32[8,128]{1,0:T(8,128)} %get-tuple-element.16.window_ref, f32[4,4]{1,0:T(4,128)} %terms_ref.3, f32[64,136,128]{2,1,0:T(8,128)} %bitcast.7, s32[4,11,16,128]{3,2,1,0:T(8,128)} %get-tuple-element.18.pick_hbm_ref, s32[16,128]{1,0:T(8,128)} %get-tuple-element.19.color_ref, ...), custom_call_target="tpu_custom_call" | custom-call | tf_op jit(solution)/shard_map/sweeps/pallas_call | solution.py:1004
  71.3 11.0 %total.1 = f32[1,4]{1,0:T(1,128)} custom-call(f32[8,128]{1,0:T(8,128)} %get-tuple-element.28.sums_ref), custom_call_target="tpu_custom_call" | custom-call | tf_op jit(solution)/shard_map/total/pallas_call | solution.py:1035
  82.3 1.1 %copy.11 = f32[4,1]{0,1:T(1,128)} copy(f32[4,1]{0,1:T(1,128)} %bitcast.15) | data formatting | bytes 32

commit v2 on v0

--- a/solution.py
+++ b/solution.py
@@ -473,9 +473,9 @@
 def gather_kernel(
     tiles, bands, obs, list_len, rows, fields,
     terms_ref, tile_lists_ref, field_colors_ref, mags_ref, wts_ref, slots_ref, owner_ref,
-    all_ref, pick_ref, color_ref, window_ref, chosen_ref, data_ref, data_places_ref, places_ref,
-    rows_ref, own_ref, listed_ref, place_ref, sorted_ref, lists_ref, data_slots_ref,
-    send_sems, recv_sems, early_send_sems, early_recv_sems,
+    out_ref, pick_ref, color_ref, window_ref, chosen_ref, data_ref, data_places_ref, places_ref,
+    all_ref, rows_ref, own_ref, listed_ref, place_ref, sorted_ref, lists_ref, data_slots_ref,
+    send_sems, recv_sems, early_send_sems, early_recv_sems, plane_send_sems, plane_recv_sems, save_sems,
 ):
     high_count = tiles // 2
     blocks = tile_lists_ref.shape[0]
@@ -604,14 +604,20 @@
         for part in (all_ref.at[:, :, 1 - side, core, 0], all_ref.at[:, 1 - low, :, core, 1]):
             late.append(send(part, part, to_core))
         wait(late)
+        save = pltpu.make_async_copy(all_ref, out_ref, save_sems.at[0])
+        save.start()
+        save.wait()
         return
 
     chunks = high_count * 8
     lower, upper = high > 0, high < high_count - 1
     own_chunk = all_ref.at[high, low, side, core]
     couple(bands, obs, list_len, rows, terms_ref, data_ref, data_places_ref, own_chunk)
+    depth = all_ref.shape[5]
+    ahead = depth // 32 * 8
+
     def copy_of(kind, z, y, x, part, peer, landing):
-        chunk = all_ref.at[z, y, x, core, part]
+        chunk = all_ref.at[z, y, x, core, part, ahead:depth]
         number = ((z * 2 + y) * 2 + x) * 2 + part
         return pltpu.make_async_remote_copy(
             src_ref=chunk,
@@ -622,6 +628,37 @@
             device_id_type=MESH,
         )
 
+    def plane_copy(chunk, number, landing, peer):
+        return pltpu.make_async_remote_copy(
+            src_ref=chunk,
+            dst_ref=chunk,
+            send_sem=plane_send_sems.at[number],
+            recv_sem=plane_recv_sems.at[landing],
+            device_id=peer,
+            device_id_type=MESH,
+        )
+
+    def head_x(y, part, number):
+        chunk = all_ref.at[high, y, side, core, part, 0:ahead]
+        return plane_copy(chunk, number, (y * 2 + side) * 2 + part, to_side)
+
+    def head_y(x, part, number):
+        chunk = all_ref.at[high, low, x, core, part, 0:ahead]
+        return plane_copy(chunk, number, (low * 2 + x) * 2 + part, to_low)
+
+    def head_arrived(y, x, part):
+        chunk = all_ref.at[high, y, x, core, part, 0:ahead]
+        plane_copy(chunk, 0, (y * 2 + x) * 2 + part, to_core).wait_recv()
+
+    def plane_along(z, step):
+        chunk = all_ref.at[z, :, :, core, :, 0:ahead]
+        number = 6 + high_count * ((step + 1) // 2) + z
+        return plane_copy(chunk, number, 8 + z, {"sky": (high + step) * 2 + low})
+
+    def plane_over(z):
+        chunk = all_ref.at[z, :, :, core, :, 0:ahead]
+        return plane_copy(chunk, 6 + 2 * high_count + z, 8 + high_count + z, to_core)
+
     def along(z, part, step):
         return copy_of((step + 1) // 2, z, low, side, part, {"sky": (high + step) * 2 + low}, 0)
 
@@ -656,14 +693,47 @@
         else:
             across_x(z, low, part).start()
 
+    head_x(low, 0, 0).start()
+    head_y(side, 1, 3).start()
     for part in range(2):
         along_if(high, part, 1)
         along_if(high, part, -1)
         first_hop(high, part)
+        if part == 0:
+            head_y(side, 0, 4).start()
+            head_x(low, 1, 1).start()
     for part in range(2):
         second_hop(high, part)
         over(high, low, side, part).start()
     tables()
+
+    def heads_turn():
+        head_arrived(low, 1 - side, 0)
+        head_y(1 - side, 0, 5).start()
+        head_arrived(1 - low, side, 1)
+        head_x(1 - low, 1, 2).start()
+
+    def send_plane(z, steps):
+        for step in steps:
+            @pl.when(ends[step])
+            def _(step=step):
+                plane_along(z, step).start()
+
+        plane_over(z).start()
+
+    def heads_done():
+        for y, x, part in ((1 - low, side, 0), (low, 1 - side, 1), (1 - low, 1 - side, 0), (1 - low, 1 - side, 1)):
+            head_arrived(y, x, part)
+        send_plane(high, (-1, 1))
+
+    def plane_arrival(distance):
+        for step in (-1, 1):
+            z = high - step * distance
+
+            @pl.when(z >= 0 if step == 1 else z < high_count)
+            def _(z=z, step=step):
+                plane_copy(all_ref.at[z, :, :, core, :, 0:ahead], 0, 8 + z, to_core).wait_recv()
+                send_plane(z, (step,))
 
     def column_arrival(distance, part):
         for step in (-1, 1):
@@ -702,23 +772,56 @@
             arrived(z, y, x, part)
             over(z, y, x, part).start()
 
+    def save(z, k):
+        return pltpu.make_async_copy(all_ref.at[z, :, :, k], out_ref.at[z, :, :, k], save_sems.at[z * 2 + k])
+
+    def save_own(z):
+        save(z, core).start()
+
+    def save_other(z):
+        for y in range(2):
+            for x in range(2):
+                for part in range(2):
+                    copy_of(4, z, y, x, part, to_core, 1).wait_recv()
+        plane_over(z).wait_recv()
+        save(z, 1 - core).start()
+
+    heads_turn()
     for distance in range(1, high_count):
         column_arrival(distance, 0)
         at_distance(distance - 1, turn)
         column_arrival(distance, 1)
-        if distance > 1:
+        if distance == 1:
+            heads_done()
+            more_tables()
+        else:
+            plane_arrival(distance - 1)
             at_distance(distance - 2, last)
-        if distance == 1:
-            more_tables()
+            at_distance(distance - 2, save_own)
     at_distance(high_count - 1, turn)
+    plane_arrival(high_count - 1)
     for distance in range(max(high_count - 2, 0), high_count):
         at_distance(distance, last)
-
+        at_distance(distance, save_own)
+    for distance in range(high_count):
+        at_distance(distance, save_other)
     for z in range(high_count):
         for y in range(2):
             for x in range(2):
                 for part in range(2):
-                    copy_of(4, z, y, x, part, to_core, 1).wait()
+                    copy_of(4, z, y, x, part, to_core, 1).wait_send()
+        plane_over(z).wait_send()
+        for step in (-1, 1):
+            passing = (z >= high) if step == -1 else (z <= high)
+
+            @pl.when(ends[step] & passing)
+            def _(z=z, step=step):
+                plane_along(z, step).wait_send()
+
+    for y, part, number in ((low, 0, 0), (low, 1, 1), (1 - low, 1, 2)):
+        head_x(y, part, number).wait_send()
+    for x, part, number in ((side, 1, 3), (side, 0, 4), (1 - side, 0, 5)):
+        head_y(x, part, number).wait_send()
     for z in range(high_count):
         for part in range(2):
             for step in (-1, 1):
@@ -735,6 +838,9 @@
                     across_x(z, other, part).wait_send()
             first = across_x(z, low, part) if part == 0 else across_y(z, side, part)
             first.wait_send()
+    for z in range(high_count):
+        for k in range(2):
+            save(z, k).wait()
 
 
 def total_kernel(tiles, bands, scale, sums_ref, misfit_ref, all_sums, send_sems, recv_sems):
@@ -810,8 +916,9 @@
             jax.ShapeDtypeStruct((obs, stars), jnp.int32),
         ),
         in_specs=[smem] + [vmem] * 6,
-        out_specs=(vmem,) * 8,
+        out_specs=(hbm,) + (vmem,) * 7,
         scratch_shapes=[
+            pltpu.VMEM(everyone, jnp.float32),
             pltpu.VMEM((row_count + 16, LANES), jnp.int32),
             pltpu.VMEM(part, jnp.float32),
             pltpu.VMEM((8, LANES), jnp.int32),
@@ -823,6 +930,9 @@
             pltpu.SemaphoreType.DMA((landings,)),
             pltpu.SemaphoreType.DMA((earlier,)),
             pltpu.SemaphoreType.DMA((earlier,)),
+            pltpu.SemaphoreType.DMA((6 + 3 * (tiles // 2),)),
+            pltpu.SemaphoreType.DMA((8 + tiles,)),
+            pltpu.SemaphoreType.DMA((tiles,)),
         ],
         compiler_params=pltpu.CompilerParams(
             collective_id=0, has_side_effects=True, vmem_limit_bytes=60 * 1024 * 1024

time: 81.5 us -> 80.8 us (level); the launches traced: 81.5 us -> 82 us
    pallas_call x1, Pallas kernels: 30.5 us -> 32.5 us  [body(): pl.pallas_call(functools.partial(sweep_kernel, tiles, bands, obs, list_le...]
    pallas_call x1, Pallas kernels: 40 us -> 38.3 us  [body(): pl.pallas_call(functools.partial(gather_kernel, tiles, bands, obs, list_l...]
where the time goes in v2:
time: 80.8 us; the launch traced here: 82 us
  Pallas kernels  80.2 us (99%)
  local copies, waits for them, and re-layouts  1.14 us (1%)
    pallas_call x1, Pallas kernels, body(): pl.pallas_call(functools.partial(gather_kernel, tiles, bands, obs, list_l...  38.3 us
    pallas_call x1, Pallas kernels, body(): pl.pallas_call(functools.partial(sweep_kernel, tiles, bands, obs, list_le...  32.5 us
    pallas_call x1, Pallas kernels, body(): pl.pallas_call(functools.partial(total_kernel, tiles, bands, float(obs *...  9.46 us

profile of v2, /device:TPU:0, one launch (start us, length us, event | category | flops | bytes accessed | tf_op | source)
XLA Modules:
  0.0 82.0 jit_solution(9983247999369936284)
XLA Ops:
  0.6 38.3 %gather.1 = (f32[4,2,2,2,2,136,128]{6,5,4,3,2,1,0:T(8,128)}, s32[4,11,16,128]{3,2,1,0:T(8,128)}, s32[16,128]{1,0:T(8,128)}, s32[8,128]{1,0:T(8,128)}, s32[4,8,12...) custom-call(f32[4,4]{1,0:T(4,128)} %terms_ref.3, s32[8,32]{1,0:T(8,128)} %tile_lists_ref.1, ...), custom_call_target="tpu_custom_call" | custom-call | tf_op jit(solution)/shard_map/gather/pallas_call | solution.py:906
  38.9 32.5 %sweeps.1 = (f32[1,512]{1,0:T(1,128)}, f32[1,2048]{1,0:T(1,128)}, f32[8,128]{1,0:T(8,128)}) custom-call(s32[8,128]{1,0:T(8,128)} %get-tuple-element.14.window_ref, f32[4,4]{1,0:T(4,128)} %terms_ref.3, f32[64,136,128]{2,1,0:T(8,128)} %bitcast.7, s32[4,11,16,128]{3,2,1,0:T(8,128)} %get-tuple-element.16.pick_ref, s32[16,128]{1,0:T(8,128)} %get-tuple-element.17.color_ref, ...), custom_call_target="tpu_custom_call" | custom-call | tf_op jit(solution)/shard_map/sweeps/pallas_call | solution.py:946
  71.4 9.5 %total.1 = f32[1,4]{1,0:T(1,128)} custom-call(f32[8,128]{1,0:T(8,128)} %get-tuple-element.24.sums_ref), custom_call_target="tpu_custom_call" | custom-call | tf_op jit(solution)/shard_map/total/pallas_call | solution.py:971
  80.9 1.1 %copy.11 = f32[4,1]{0,1:T(1,128)} copy(f32[4,1]{0,1:T(1,128)} %bitcast.15) | data formatting | bytes 32

commit v3 on v2

--- a/solution.py
+++ b/solution.py
@@ -165,21 +165,32 @@
                     sums[index] = sums[index] + jnp.where(mask, take(near[band], lanes), 0.0)
         return sums
 
-    def gathered(group):
-        sums = []
-        for band in range(bands):
-            sums += [tot[band, pl.ds(pl.multiple_of(group * 8 + 8, 8), 8), :], jnp.zeros((8, LANES), jnp.float32)]
-        sums = gather(group, 0, 2, sums)
-        sums = lax.fori_loop(2, window_ref[0, 2], lambda level, sums: gather(group, level, 1, sums), sums)
-        return [sums[2 * band] + sums[2 * band + 1] for band in range(bands)]
-
-    def weigh(group, carry):
-        for band, value in enumerate(gathered(group)):
-            rden[band, rows_of(group), :] = 1.0 / (value + PRIOR_WEIGHT)
+    span = 2 if groups % 2 == 0 else 1
+
+    def gathered(batch):
+        around = [batch * span + part for part in range(span)]
+        first = []
+        for group in around:
+            sums = []
+            for band in range(bands):
+                middle = pl.ds(pl.multiple_of(group * 8 + 8, 8), 8)
+                sums += [tot[band, middle, :], jnp.zeros((8, LANES), jnp.float32)]
+            first.append(gather(group, 0, 2, sums))
+
+        def deeper(level, sums):
+            return [gather(group, level, 1, part) for group, part in zip(around, sums)]
+
+        result = lax.fori_loop(2, window_ref[0, 2], deeper, first)
+        return [(group, [part[2 * b] + part[2 * b + 1] for b in range(bands)]) for group, part in zip(around, result)]
+
+    def weigh(batch, carry):
+        for group, values in gathered(batch):
+            for band, value in enumerate(values):
+                rden[band, rows_of(group), :] = 1.0 / (value + PRIOR_WEIGHT)
         return carry
 
     wrap()
-    lax.fori_loop(0, groups, weigh, 0)
+    lax.fori_loop(0, groups // span, weigh, 0)
     zp[...] = jnp.zeros_like(zp)
     tot[:, 8 : row_count + 8, :] = base[...]
     wrap()
@@ -238,26 +249,28 @@
     def step(number, carry):
         color_no = lax.rem(number, COLORS)
 
-        def update(group, inner):
-            rows = rows_of(group)
-            now = color_ref[rows, :] == color_no
-            for band, value in enumerate(gathered(group)):
-                old = zp[band, rows, :]
-                new = jnp.where(now, value * rden[band, rows, :], old)
-                zp[band, rows, :] = new
-                move[band, rows, :] = new - old
+        def update(batch, inner):
+            for group, values in gathered(batch):
+                rows = rows_of(group)
+                now = color_ref[rows, :] == color_no
+                for band, value in enumerate(values):
+                    old = zp[band, rows, :]
+                    new = jnp.where(now, value * rden[band, rows, :], old)
+                    zp[band, rows, :] = new
+                    move[band, rows, :] = new - old
             return inner
 
-        lax.fori_loop(0, groups, update, 0, unroll=2)
+        lax.fori_loop(0, groups // span, update, 0)
 
         @pl.when(color_no == COLORS - 1)
         def _():
             misfit_lines(lax.div(number, COLORS))
 
         low, high = window_ref[color_no, 0], window_ref[color_no, 1]
-        widths = (list_len // 4, list_len * 3 // 8, list_len // 2)
+        widths = [list_len * eighths // 16 for eighths in range(4, 9)]
+        more = number < SWEEPS * COLORS - 1
         for index, width in enumerate(widths):
-            fits = high - low <= width
+            fits = more & (high - low <= width)
             if index:
                 fits = fits & (high - low > widths[index - 1])
 
@@ -265,7 +278,7 @@
             def _(width=width):
                 push(width, jnp.minimum(low, list_len - width))
 
-        @pl.when(high - low > widths[-1])
+        @pl.when(more & (high - low > widths[-1]))
         def _():
             lax.fori_loop(0, 2, lambda part, inner: (push(widths[-1], part * widths[-1]), inner)[1], 0)
 

time: 80.8 us -> 78.4 us (0.970); the launches traced: 82 us -> 78.1 us
  Pallas kernels: 80.2 us -> 76.3 us
    pallas_call x1, Pallas kernels: 32.5 us -> 28.6 us  [body(): pl.pallas_call(functools.partial(sweep_kernel, tiles, bands, obs, list_le...]
where the time goes in v3:
time: 78.4 us; the launch traced here: 78.1 us
  Pallas kernels  76.3 us (97%)
  local copies, waits for them, and re-layouts  1.14 us (1%)
    pallas_call x1, Pallas kernels, body(): pl.pallas_call(functools.partial(gather_kernel, tiles, bands, obs, list_l...  38.3 us
    pallas_call x1, Pallas kernels, body(): pl.pallas_call(functools.partial(sweep_kernel, tiles, bands, obs, list_le...  28.6 us
    pallas_call x1, Pallas kernels, body(): pl.pallas_call(functools.partial(total_kernel, tiles, bands, float(obs *...  9.46 us

profile of v3, /device:TPU:0, one launch (start us, length us, event | category | flops | bytes accessed | tf_op | source)
XLA Modules:
  0.0 78.1 jit_solution(6920491819746349861)
XLA Ops:
  0.6 38.3 %gather.1 = (f32[4,2,2,2,2,136,128]{6,5,4,3,2,1,0:T(8,128)}, s32[4,11,16,128]{3,2,1,0:T(8,128)}, s32[16,128]{1,0:T(8,128)}, s32[8,128]{1,0:T(8,128)}, s32[4,8,12...) custom-call(f32[4,4]{1,0:T(4,128)} %terms_ref.3, s32[8,32]{1,0:T(8,128)} %tile_lists_ref.1, ...), custom_call_target="tpu_custom_call" | custom-call | tf_op jit(solution)/shard_map/gather/pallas_call | solution.py:919
  38.9 28.6 %sweeps.1 = (f32[1,512]{1,0:T(1,128)}, f32[1,2048]{1,0:T(1,128)}, f32[8,128]{1,0:T(8,128)}) custom-call(s32[8,128]{1,0:T(8,128)} %get-tuple-element.14.window_ref, f32[4,4]{1,0:T(4,128)} %terms_ref.3, f32[64,136,128]{2,1,0:T(8,128)} %bitcast.7, s32[4,11,16,128]{3,2,1,0:T(8,128)} %get-tuple-element.16.pick_ref, s32[16,128]{1,0:T(8,128)} %get-tuple-element.17.color_ref, ...), custom_call_target="tpu_custom_call" | custom-call | tf_op jit(solution)/shard_map/sweeps/pallas_call | solution.py:959
  67.5 9.5 %total.1 = f32[1,4]{1,0:T(1,128)} custom-call(f32[8,128]{1,0:T(8,128)} %get-tuple-element.24.sums_ref), custom_call_target="tpu_custom_call" | custom-call | tf_op jit(solution)/shard_map/total/pallas_call | solution.py:984
  77.0 1.1 %copy.11 = f32[4,1]{0,1:T(1,128)} copy(f32[4,1]{0,1:T(1,128)} %bitcast.15) | data formatting | bytes 32
